TPU v7x, 256 devices: a whole 4x4x8 slice. The times are simulated.
256 devices in a mesh: section: 2 (over core), rep: 8 (over z_lo, x), tp: 16 (over z_hi, y).
Axes of the slice: x: 4, y: 4, z: 8 (z_hi: 4, z_lo: 2; z = z_hi * 2 + z_lo), core: 2. Of those that a mesh axis runs over, the one named last changes fastest.
Arguments:
- states: bfloat16 [2, 8, 256, 8192], P('section', 'rep', None, 'tp'), may hold values from -6 to 6
- q_weight: bfloat16 [8192, 4096], P(None, 'tp'), may hold values from -0.0625 to 0.0625
- kv_weight: bfloat16 [8192, 1024], P('tp'), may hold values from -0.0625 to 0.0625
- o_weight: bfloat16 [4096, 8192], P(None, 'tp'), may hold values from -0.09375 to 0.09375
- store_keys: bfloat16 [2, 8, 4096, 512], P('section', 'rep', 'tp'), may hold values from -170 to 170
- store_values: bfloat16 [2, 8, 4096, 512], P('section', 'rep', 'tp'), may hold values from -48 to 48
- prefix_len: int32 [8], replicated, may hold values from 1024 to 4096
- cache_len: int32 [8, 4], P('rep'), may hold values from 128 to 1024
- parents: int32 [8, 4, 64], P('rep'), may hold values from -1 to 62, as said below
Outputs:
- attn_out: bfloat16 [2, 8, 256, 8192], P('section', 'rep', None, 'tp')
Inputs may be any that keep to these rules, and one draw needn't show every extreme that they name: `parents`: each node's parent is an earlier node of the same tree; only node 0 has -1.
All inputs are finite; a program needn't handle non-finite values.
Results may differ from a plain program's by a relative error of at most 0.0065.
The roundings to bfloat16 on the way count: a program that leaves them out, or rounds other values in their place, can miss the bound.
Values may be sent and summed in bfloat16 or wider, within the bound.
A program may use at most 64 MiB of HBM per device.

v0:
```python
import jax
import jax.numpy as jnp
from jax import lax
from jax.sharding import Mesh
from jax.sharding import PartitionSpec as P

HD = 128
SEQS = 4
NODES = 64
CACHE = 1024
TP = ("tp_0", "tp_1")
ROPE_BASE = 500000.0
MASKED_SCORE = -1e30


def in_blocks(shard, dim, devices):
    before, after = (shard.shape[:dim], shard.shape[dim + 1 :])
    return jnp.moveaxis(shard.reshape(*before, devices, -1, *after), dim, 0)


def summed_on_arrival(shard, axis, dim):
    tiles = in_blocks(shard, dim, lax.axis_size(axis))
    arrived = lax.all_to_all(tiles, axis, split_axis=0, concat_axis=0, tiled=True)
    return arrived.astype(jnp.float32).sum(axis=0)


def passed_along(block, axis, distance):
    devices = range(lax.axis_size(axis))
    route = [(i - distance, i) for i in devices if i - distance in devices]
    return lax.ppermute(block, axis, route)


def joined_along(tiles, dim):
    lengths = list(tiles.shape[1:])
    lengths[dim] *= tiles.shape[0]
    return jnp.moveaxis(tiles, 0, dim).reshape(lengths)


def exchange_in_order(tiles, axes, order):
    lengths = [lax.axis_size(a) for a in axes]
    tiles = tiles.reshape(*lengths, *tiles.shape[1:])
    for k in order:
        tiles = lax.all_to_all(tiles, axes[k], split_axis=k, concat_axis=k, tiled=True)
    return tiles.reshape(-1, *tiles.shape[len(axes) :])


def exchange_by_axis(shard, axes, order, split_dim, concat_dim):
    tiles = in_blocks(shard, split_dim, lax.axis_size(axes))
    return joined_along(exchange_in_order(tiles, axes, order), concat_dim)


def rotate(vectors, positions):
    head_size = vectors.shape[-1]
    half_width = head_size // 2
    exponent = jnp.arange(half_width, dtype=jnp.float32) * (-2.0 / head_size)
    frequency = jnp.exp(exponent * jnp.log(jnp.float32(ROPE_BASE)))
    angles = positions.astype(jnp.float32)[:, None] * frequency[None, :]
    cosine = jnp.cos(angles)[:, None, :]
    sine_of = jnp.sin(angles)[:, None, :]
    front_half = vectors[..., :half_width]
    back_half = vectors[..., half_width:]
    return jnp.concatenate(
        [front_half * cosine - back_half * sine_of, back_half * cosine + front_half * sine_of],
        axis=-1,
    )


def closure(parents):
    node_count = parents.shape[-1]
    node_ids = jnp.arange(node_count, dtype=jnp.int32)
    reached = (parents[:, :, None] == node_ids[None, None, :]).astype(jnp.float32)
    reached = reached + jnp.eye(node_count, dtype=jnp.float32)[None]
    for level_index in range(max(1, (node_count - 1).bit_length())):
        reached = jnp.minimum(
            jnp.einsum("sij,sjk->sik", reached, reached, precision=lax.Precision.HIGHEST), 1.0
        )
    return reached


def partial_attend(queries, all_keys, all_values, visible):
    row_count = queries.shape[0]
    kv_heads = all_keys.shape[1] // HD
    group_size = queries.shape[1] // all_keys.shape[1]
    row_tops = []
    row_totals = []
    mixtures = []
    for kv_head in range(kv_heads):
        query_block = queries[
            :, kv_head * group_size * HD : (kv_head + 1) * group_size * HD
        ].reshape(row_count * group_size, HD)
        key_block = all_keys[:, kv_head * HD : (kv_head + 1) * HD]
        value_block = all_values[:, kv_head * HD : (kv_head + 1) * HD]
        scores = lax.dot_general(
            query_block, key_block, (((1,), (1,)), ((), ())), preferred_element_type=jnp.float32
        )
        scores = scores.reshape(row_count, group_size, -1) * HD ** (-0.5)
        scores = jnp.where(visible[:, None, :], scores, MASKED_SCORE)
        row_top = jnp.max(scores, axis=-1)
        weights = jnp.where(visible[:, None, :], jnp.exp(scores - row_top[..., None]), 0.0)
        row_total = jnp.sum(weights, axis=-1)
        mixed_rows = jnp.dot(
            weights.astype(jnp.bfloat16).reshape(row_count * group_size, -1),
            value_block,
            preferred_element_type=jnp.float32,
        )
        mixed_rows = (
            mixed_rows.reshape(row_count, group_size, HD) / jnp.maximum(row_total, 1.0)[..., None]
        )
        row_tops.append(row_top)
        row_totals.append(row_total)
        mixtures.append(mixed_rows.reshape(row_count, group_size * HD).astype(jnp.bfloat16))
    return (
        jnp.concatenate(row_tops, axis=1),
        jnp.concatenate(row_totals, axis=1),
        jnp.concatenate(mixtures, axis=1),
    )


def finish(tops, totals, parts):
    piece_count, row_count, head_count = tops.shape
    best = jnp.max(tops, axis=0)
    factor = jnp.exp(tops - best[None]) * totals
    denominator = jnp.sum(factor, axis=0)
    numerator = jnp.sum(
        parts.astype(jnp.float32).reshape(piece_count, row_count, head_count, HD)
        * factor[..., None],
        axis=0,
    )
    return (
        (numerator / denominator[..., None])
        .reshape(row_count, head_count * HD)
        .astype(jnp.bfloat16)
    )


def per_device(
    states, q_weight, kv_weight, o_weight, store_keys, store_values, prefix_len, cache_len, parents
):
    inputs = states[0, 0]
    row_count = inputs.shape[0]
    tp_count = lax.axis_size(TP)
    tp_index = lax.axis_index(TP)
    replica = lax.axis_index("rep")
    rep_count = lax.axis_size("rep")
    decoding = lax.axis_index("section") == 1
    own_cols = q_weight.shape[1]
    kv_width = kv_weight.shape[1] // 2
    block_rows = row_count // tp_count
    first_row = tp_index * block_rows
    row_ids = jnp.arange(row_count, dtype=jnp.int32)
    seq_of = row_ids // NODES
    own_prefix = prefix_len[replica]
    reached = closure(parents[0])
    depths = (jnp.sum(reached, axis=-1).astype(jnp.int32) - 1).reshape(row_count)
    seq_lengths = jnp.broadcast_to(cache_len[0][:, None], (SEQS, NODES)).reshape(row_count)
    tree_base = jnp.where(seq_of == 0, own_prefix + row_count, seq_lengths)
    positions = jnp.where(decoding, tree_base + depths, own_prefix + row_ids)
    weight_rows = q_weight
    query_sums = jnp.dot(
        lax.all_gather(inputs, TP, axis=1, tiled=True),
        weight_rows,
        preferred_element_type=jnp.float32,
    )
    own_queries = (
        rotate(query_sums.reshape(row_count, own_cols // HD, HD), positions)
        .reshape(row_count, own_cols)
        .astype(jnp.bfloat16)
    )
    queries = lax.all_gather(own_queries, TP, axis=1, tiled=True)
    kv_rows = summed_on_arrival(
        jnp.dot(inputs, kv_weight, preferred_element_type=jnp.float32).astype(jnp.bfloat16), TP, 0
    )
    local_pos = lax.dynamic_slice_in_dim(positions, first_row, block_rows, 0)
    new_keys = (
        rotate(kv_rows[:, :kv_width].reshape(block_rows, -1, HD), local_pos)
        .reshape(block_rows, kv_width)
        .astype(jnp.bfloat16)
    )
    new_values = kv_rows[:, kv_width:].astype(jnp.bfloat16)
    moved = passed_along(jnp.stack([new_keys, new_values]), ("section", "rep"), rep_count)
    tail_keys = moved[0]
    tail_values = moved[1]
    store_rows = store_keys.shape[2]
    store_pos = tp_index * store_rows + jnp.arange(store_rows, dtype=jnp.int32)
    prefill_store = jnp.broadcast_to(store_pos[None, :] < own_prefix, (row_count, store_rows))
    decode_store = (store_pos[None, :] // CACHE == seq_of[:, None]) & (
        store_pos[None, :] % CACHE < seq_lengths[:, None]
    )
    block_ids = first_row + jnp.arange(block_rows, dtype=jnp.int32)
    prefill_new = block_ids[None, :] <= row_ids[:, None]
    eye_seq = (jnp.arange(SEQS)[:, None] == jnp.arange(SEQS)[None, :]).astype(jnp.float32)
    tree_full = (eye_seq[:, None, :, None] * reached[:, :, None, :]).reshape(row_count, row_count)
    decode_new = lax.dynamic_slice_in_dim(tree_full, first_row, block_rows, 1) > 0.5
    tail_seen = jnp.broadcast_to((seq_of == 0)[:, None], (row_count, block_rows))
    decode_mask = jnp.concatenate([decode_store, decode_new, tail_seen], axis=1)
    prefill_mask = jnp.concatenate([prefill_store, prefill_new, jnp.zeros_like(tail_seen)], axis=1)
    visible = jnp.where(decoding, decode_mask, prefill_mask)
    all_keys = jnp.concatenate([store_keys[0, 0], new_keys, tail_keys], axis=0)
    all_values = jnp.concatenate([store_values[0, 0], new_values, tail_values], axis=0)
    row_tops, row_totals, mixtures = partial_attend(queries, all_keys, all_values, visible)
    peer_tops, peer_totals, peer_mix = (
        exchange_by_axis(row_tops[None], TP, (0, 1), 2, 0),
        exchange_by_axis(row_totals[None], TP, (0, 1), 2, 0),
        exchange_by_axis(mixtures[None].astype(jnp.float32), TP, (0, 1), 2, 0).astype(jnp.bfloat16),
    )
    own_attended = finish(peer_tops, peer_totals, peer_mix)
    weight_rows = o_weight
    result = jnp.dot(
        lax.all_gather(own_attended, TP, axis=1, tiled=True),
        weight_rows,
        preferred_element_type=jnp.float32,
    )
    return result.astype(jnp.bfloat16)[None, None]


def solution(mesh):
    split = Mesh(
        mesh.devices.reshape(mesh.shape["section"], mesh.shape["rep"], 4, 4),
        ("section", "rep", "tp_0", "tp_1"),
    )
    placed = (
        P("section", "rep", None, TP),
        P(None, TP),
        P(TP, None),
        P(None, TP),
        P("section", "rep", TP, None),
        P("section", "rep", TP, None),
        P(),
        P("rep", None),
        P("rep", None, None),
    )
    return jax.shard_map(
        per_device,
        mesh=split,
        in_specs=placed,
        out_specs=P("section", "rep", None, TP),
        check_vma=False,
    )
```

profile of v0, /device:TPU:2, one launch (start us, length us, event | category | flops | bytes accessed | tf_op | source)
XLA Modules:
  0.0 364.5 jit_solution(4483975345601718534)
XLA Ops:
  6.5 0.7 all-gather.9.cloned.1.call-update
  7.3 0.7 broadcast_in_dim.55
  8.1 1.1 convolution_minimum_fusion.5
  9.3 0.3 convolution_minimum_fusion.4
  9.5 0.3 convolution_minimum_fusion.3
  9.8 0.3 convolution_minimum_fusion.2
  10.0 0.3 convolution_minimum_fusion.1
  10.3 0.4 fusion.72
  10.8 0.7 dynamic_slice.10
  12.1 0.7 fusion.70
  12.8 0.3 multiply_cosine_fusion
  13.1 81.5 %all-gather.9.cloned.1.call-done = bf16[1,1,256,8192]{3,2,1,0:T(8,128)(2,1)} async-done(((bf16[1,1,256,512]{3,2,1,0:T(8,128)(2,1)}), bf16[1,1,256,8192]{3,2,1,0:T(8,128)(2,1)}) %all-gather.9.cloned.1.call-update) | async-done | bytes 4194320 | tf_op jit(solution)/shard_map/all_gather | solution.py:160
  94.6 5.2 %fusion = f32[256,256]{0,1:T(8,128)S(1)} fusion(bf16[8192,256]{1,0:T(8,128)(2,1)} %param.10, bf16[1,1,256,8192]{3,2,1,0:T(8,128)(2,1)} %all-gather.9.cloned.1.call-done), kind=kOutput, calls=%fused_computation | convolution fusion | flops 1073741824 | bytes 8650752 | tf_op jit(solution)/shard_map/dot_general | solution.py:159
  99.9 0.7 pad_maximum_fusion.2
  100.6 1.2 convolution_convert_fusion
  101.8 6.2 %all-to-all-start = ((bf16[16,16,1024]{2,1,0:T(8,128)(2,1)}), bf16[16,16,1024]{2,1,0:T(8,128)(2,1)S(1)}, u32[]{:S(2)}, u32[]{:S(2)}) async-start(bf16[16,16,1024]{2,1,0:T(8,128)(2,1)} %bitcast.9), calls=%async_computation | async-start | bytes 1048576 | tf_op jit(solution)/shard_map/all_to_all | solution.py:23
  108.1 0.7 fusion.56
  108.9 0.1 copy.33
  109.0 0.1 broadcast_multiply_fusion
  109.2 0.3 mul.174
  109.7 0.1 multiply_cosine_fusion.1
  109.8 0.1 compare_and_fusion
  110.0 18.6 %all-to-all-done = bf16[16,16,1024]{2,1,0:T(8,128)(2,1)S(1)} async-done(((bf16[16,16,1024]{2,1,0:T(8,128)(2,1)}), bf16[16,16,1024]{2,1,0:T(8,128)(2,1)S(1)}, u32[]{:S(2)}, u32[]{:S(2)}) %all-to-all-start) | async-done | bytes 524320 | tf_op jit(solution)/shard_map/all_to_all | solution.py:23
  128.7 0.1 multiply_subtract_fusion
  128.8 0.1 maximum_convert_fusion.1
  128.9 1.3 collective-permute-start
  130.2 0.1 add_select_fusion
  130.4 0.6 collective-permute-done
  131.1 0.9 pad_maximum_fusion
  131.9 31.4 %all-gather.5.cloned.1.call-done = bf16[256,4096]{0,1:T(8,128)(2,1)} async-done(((bf16[256,256]{0,1:T(8,128)(2,1)}), bf16[256,4096]{0,1:T(8,128)(2,1)}) %all-gather.5.cloned.1.call-update) | async-done | bytes 2097168 | tf_op jit(solution)/shard_map/all_gather | solution.py:169
  163.3 1.7 fusion.71
  165.0 0.5 fusion.47
  165.5 0.5 fusion.48
  166.0 0.5 fusion.2
  166.5 3.3 fusion.6
  169.8 0.6 broadcast_maximum_fusion.3
  170.4 0.6 reshape_broadcast_in_dim.6
  171.0 4.7 %all-to-all-start.3 = ((f32[4,4,1,256,2]{3,4,1,2,0:T(2,128)}), f32[4,4,1,256,2]{3,4,1,2,0:T(2,128)S(1)}, u32[]{:S(2)}, u32[]{:S(2)}) async-start(f32[4,4,1,256,2]{3,4,1,2,0:T(2,128)} %bitcast.32), calls=%async_computation.3 | async-start | bytes 65536 | tf_op jit(solution)/shard_map/all_to_all | solution.py:43
  175.7 4.3 %fusion.8 = (f32[256,8]{0,1:T(8,128)S(1)}, f32[256,8]{0,1:T(8,128)S(1)}, f32[256,8]{0,1:T(8,128)S(1)}) fusion(f32[256,8,288]{0,2,1:T(8,128)} %get-tuple-element.32, f32[256,8]{0,1:T(8,128)S(1)} %get-tuple-element.6, pred[256,288]{0,1:T(8,128)(4,1)S(1)} %add_select_fusion, f32[256,8]{0,1:T(8,128)S(1)} %get-tuple-element.7, f32[256,8,288]{0,2,1:T(8,128)} %copy-done.1, ...), kind=kLoop, calls=%fused_computation.19 | loop fusion | flops 8841216 | bytes 7200768 | tf_op jit(solution)/shard_map/reduce_sum | solution.py:100
  180.0 1.6 fusion.14
  181.7 1.6 fusion.15
  183.3 1.6 fusion.16
  184.9 0.6 broadcast_maximum_fusion
  185.5 0.6 reshape_broadcast_in_dim.7
  186.2 7.2 %all-to-all-start.5 = ((f32[4,4,1,256,2]{3,4,1,2,0:T(2,128)}), f32[4,4,1,256,2]{3,4,1,2,0:T(2,128)S(1)}, u32[]{:S(2)}, u32[]{:S(2)}) async-start(f32[4,4,1,256,2]{3,4,1,2,0:T(2,128)} %bitcast.123), calls=%async_computation.5 | async-start | bytes 65536 | tf_op jit(solution)/shard_map/all_to_all | solution.py:43
  193.3 2.5 fusion.17
  195.8 0.6 copy.40
  196.4 4.8 %all-to-all-done.5 = f32[4,4,1,256,2]{3,4,1,2,0:T(2,128)S(1)} async-done(((f32[4,4,1,256,2]{3,4,1,2,0:T(2,128)}), f32[4,4,1,256,2]{3,4,1,2,0:T(2,128)S(1)}, u32[]{:S(2)}, u32[]{:S(2)}) %all-to-all-start.5) | async-done | bytes 32800 | tf_op jit(solution)/shard_map/all_to_all | solution.py:43
  201.2 3.4 all-to-all-start.4
  204.6 3.1 maximum_convert_fusion
  207.7 2.3 all-to-all-done.4
  210.0 3.6 all-to-all-start.1
  213.7 0.6 copy.42
  214.3 45.5 %all-to-all-done.1 = bf16[4,4,1,256,256]{3,4,1,2,0:T(8,128)(2,1)S(1)} async-done(((bf16[4,4,1,256,256]{3,4,1,2,0:T(8,128)(2,1)}), bf16[4,4,1,256,256]{3,4,1,2,0:T(8,128)(2,1)S(1)}, u32[]{:S(2)}, u32[]{:S(2)}) %all-to-all-start.1) | async-done | bytes 2097184 | tf_op jit(solution)/shard_map/all_to_all | solution.py:43
  259.8 3.4 all-to-all-start.6
  263.1 1.5 copy.38
  264.6 4.0 %all-to-all-done.6 = f32[4,4,1,256,2]{3,4,0,2,1:T(2,128)S(1)} async-done(((f32[4,4,1,256,2]{3,4,0,2,1:T(2,128)}), f32[4,4,1,256,2]{3,4,0,2,1:T(2,128)S(1)}, u32[]{:S(2)}, u32[]{:S(2)}) %all-to-all-start.6) | async-done | bytes 32800 | tf_op jit(solution)/shard_map/all_to_all | solution.py:43
  268.6 3.6 all-to-all-start.2
  272.4 22.8 %all-to-all-done.2 = bf16[4,4,1,256,256]{3,4,0,2,1:T(8,128)(2,1)S(1)} async-done(((bf16[4,4,1,256,256]{3,4,0,2,1:T(8,128)(2,1)}), bf16[4,4,1,256,256]{3,4,0,2,1:T(8,128)(2,1)S(1)}, u32[]{:S(2)}, u32[]{:S(2)}) %all-to-all-start.2) | async-done | bytes 2097184 | tf_op jit(solution)/shard_map/all_to_all | solution.py:43
  295.2 0.3 mul.201
  295.5 0.5 multiply_reduce_fusion
  296.0 0.7 fusion.43
  296.7 56.5 %all-gather.7.cloned.1.call-done = bf16[256,4096]{0,1:T(8,128)(2,1)} async-done(((bf16[256,256]{0,1:T(8,128)(2,1)}), bf16[256,4096]{0,1:T(8,128)(2,1)}) %all-gather.7.cloned.1.call-update) | async-done | bytes 2097168 | tf_op jit(solution)/shard_map/all_gather | solution.py:209
  353.2 4.8 %fusion.42 = bf16[1,1,256,512]{3,2,1,0:T(8,128)(2,1)} fusion(bf16[256,4096]{0,1:T(8,128)(2,1)} %all-gather.7.cloned.1.call-done, bf16[4096,512]{1,0:T(8,128)(2,1)} %param.12), kind=kOutput, calls=%fused_computation.55 | convolution fusion | flops 1073872896 | bytes 6553600 | tf_op jit(solution)/shard_map/dot_general | solution.py:208
  (69 shorter events, 1.1 us)
Async XLA Ops:
  6.5 94.0 %copy-start = (bf16[512,1024]{1,0:T(8,128)(2,1)S(1)}, bf16[512,1024]{1,0:T(8,128)(2,1)}, u32[]{:S(2)}) copy-start(bf16[512,1024]{1,0:T(8,128)(2,1)} %param.11) | copy-start | bytes 3145732
  6.5 4.2 %copy-start.13 = (s32[8]{0:T(128)S(1)}, s32[8]{0:T(128)}, u32[]{:S(2)}) copy-start(s32[8]{0:T(128)} %param.15) | copy-start | bytes 100
  6.5 88.1 %all-gather.9.cloned.1.call-start = ((), (), s32[]{:S(2)}) async-start(), calls=%async_computation.9 | async-start | bytes 4456448 | tf_op jit(solution)/shard_map/all_gather | solution.py:160
  7.3 156.1 %all-gather.5.cloned.1.call-start = ((), (), s32[]{:S(2)}) async-start(), calls=%async_computation.7 | async-start | bytes 2228224 | tf_op jit(solution)/shard_map/all_gather | solution.py:169
  13.1 87.5 %copy-start.6 = (bf16[1,1,256,512]{3,2,1,0:T(8,128)(2,1)S(1)}, bf16[1,1,256,512]{3,2,1,0:T(8,128)(2,1)}, u32[]{:S(2)}) copy-start(bf16[1,1,256,512]{3,2,1,0:T(8,128)(2,1)} %param.9) | copy-start | bytes 786436
  101.8 29.2 %copy-start.9 = (bf16[1,1,256,512]{3,2,1,0:T(8,128)(2,1)S(1)}, bf16[1,1,256,512]{3,2,1,0:T(8,128)(2,1)}, u32[]{:S(2)}) copy-start(bf16[1,1,256,512]{3,2,1,0:T(8,128)(2,1)} %param.13) | copy-start | bytes 786436
  101.8 29.2 %copy-start.10 = (bf16[1,1,256,512]{3,2,1,0:T(8,128)(2,1)S(1)}, bf16[1,1,256,512]{3,2,1,0:T(8,128)(2,1)}, u32[]{:S(2)}) copy-start(bf16[1,1,256,512]{3,2,1,0:T(8,128)(2,1)} %param.14) | copy-start | bytes 786436
  101.8 26.7 %all-to-all-start = ((bf16[16,16,1024]{2,1,0:T(8,128)(2,1)}), bf16[16,16,1024]{2,1,0:T(8,128)(2,1)S(1)}, u32[]{:S(2)}, u32[]{:S(2)}) async-start(bf16[16,16,1024]{2,1,0:T(8,128)(2,1)} %bitcast.9), calls=%async_computation | async-start | bytes 1048576 | tf_op jit(solution)/shard_map/all_to_all | solution.py:23
  128.9 2.1 collective-permute-start
  163.3 1.7 copy-start.7
  166.0 3.8 %copy-start.1 = (f32[256,8,288]{0,2,1:T(8,128)}, f32[256,8,288]{0,2,1:T(8,128)S(1)}, u32[]{:S(2)}) copy-start(f32[256,8,288]{0,2,1:T(8,128)S(1)} %fusion.48) | copy-start | bytes 7077892
  166.5 3.3 copy-start.3
  169.8 10.2 %copy-start.11 = (f32[256,8]{0,1:T(8,128)}, f32[256,8]{0,1:T(8,128)S(1)}, u32[]{:S(2)}) copy-start(f32[256,8]{0,1:T(8,128)S(1)} %get-tuple-element.8) | copy-start | bytes 24580
  171.0 15.2 %all-to-all-start.3 = ((f32[4,4,1,256,2]{3,4,1,2,0:T(2,128)}), f32[4,4,1,256,2]{3,4,1,2,0:T(2,128)S(1)}, u32[]{:S(2)}, u32[]{:S(2)}) async-start(f32[4,4,1,256,2]{3,4,1,2,0:T(2,128)} %bitcast.32), calls=%async_computation.3 | async-start | bytes 65536 | tf_op jit(solution)/shard_map/all_to_all | solution.py:43
  175.6 4.3 %copy-start.4 = (f32[256,8,288]{0,2,1:T(8,128)S(1)}, f32[256,8,288]{0,2,1:T(8,128)}, u32[]{:S(2)}) copy-start(f32[256,8,288]{0,2,1:T(8,128)} %copy-done.3) | copy-start | bytes 7077892
  175.7 4.3 %copy-start.8 = (bf16[288,512]{1,0:T(8,128)(2,1)S(1)}, bf16[288,512]{1,0:T(8,128)(2,1)}, u32[]{:S(2)}) copy-start(bf16[288,512]{1,0:T(8,128)(2,1)} %get-tuple-element.38) | copy-start | bytes 884740
  175.7 4.3 %copy-start.12 = (f32[256,8]{0,1:T(8,128)S(1)}, f32[256,8]{0,1:T(8,128)}, u32[]{:S(2)}) copy-start(f32[256,8]{0,1:T(8,128)} %broadcast_maximum_fusion.3) | copy-start | bytes 24580
  180.0 1.7 copy-start.5
  181.7 1.7 copy-start.2
  186.2 15.1 %all-to-all-start.5 = ((f32[4,4,1,256,2]{3,4,1,2,0:T(2,128)}), f32[4,4,1,256,2]{3,4,1,2,0:T(2,128)S(1)}, u32[]{:S(2)}, u32[]{:S(2)}) async-start(f32[4,4,1,256,2]{3,4,1,2,0:T(2,128)} %bitcast.123), calls=%async_computation.5 | async-start | bytes 65536 | tf_op jit(solution)/shard_map/all_to_all | solution.py:43
  201.2 8.8 %all-to-all-start.4 = ((f32[4,4,1,256,2]{3,4,0,2,1:T(2,128)}), f32[4,4,1,256,2]{3,4,0,2,1:T(2,128)S(1)}, u32[]{:S(2)}, u32[]{:S(2)}) async-start(f32[4,4,1,256,2]{3,4,0,2,1:T(2,128)} %copy.40), calls=%async_computation.4 | async-start | bytes 65536 | tf_op jit(solution)/shard_map/all_to_all | solution.py:43
  210.0 49.7 %all-to-all-start.1 = ((bf16[4,4,1,256,256]{3,4,1,2,0:T(8,128)(2,1)}), bf16[4,4,1,256,256]{3,4,1,2,0:T(8,128)(2,1)S(1)}, u32[]{:S(2)}, u32[]{:S(2)}) async-start(bf16[4,4,1,256,256]{3,4,1,2,0:T(8,128)(2,1)} %bitcast.109), calls=%async_computation.1 | async-start | bytes 4194304 | tf_op jit(solution)/shard_map/all_to_all | solution.py:43
  259.8 8.8 %all-to-all-start.6 = ((f32[4,4,1,256,2]{3,4,0,2,1:T(2,128)}), f32[4,4,1,256,2]{3,4,0,2,1:T(2,128)S(1)}, u32[]{:S(2)}, u32[]{:S(2)}) async-start(f32[4,4,1,256,2]{3,4,0,2,1:T(2,128)} %copy.42), calls=%async_computation.6 | async-start | bytes 65536 | tf_op jit(solution)/shard_map/all_to_all | solution.py:43
  268.6 26.6 %all-to-all-start.2 = ((bf16[4,4,1,256,256]{3,4,0,2,1:T(8,128)(2,1)}), bf16[4,4,1,256,256]{3,4,0,2,1:T(8,128)(2,1)S(1)}, u32[]{:S(2)}, u32[]{:S(2)}) async-start(bf16[4,4,1,256,256]{3,4,0,2,1:T(8,128)(2,1)} %copy.38), calls=%async_computation.2 | async-start | bytes 4194304 | tf_op jit(solution)/shard_map/all_to_all | solution.py:43
  272.2 81.0 %all-gather.7.cloned.1.call-start = ((), (), s32[]{:S(2)}) async-start(), calls=%async_computation.8 | async-start | bytes 2228224 | tf_op jit(solution)/shard_map/all_gather | solution.py:209
Sparse Core Ops, SparseCore 0:
  9.7 84.8 all-gather.8
  100.7 62.5 all-gather.4
  296.9 56.3 all-gather.6
where the time goes:
time: 365 us
  waiting for transfers between devices  269 us (74%)
  starting transfers between devices  33.4 us (9%)
  matrix products  25.7 us (7%)
  between operations  14.2 us (4%)
  other arithmetic  14.1 us (4%)
  local copies, waits for them, and re-layouts  8.3 us (2%)
    all_gather x1, waiting for transfers between devices, per_device(): lax.all_gather(inputs, TP, axis=1, tiled=True)  81.5 us
    all_to_all x6, waiting for transfers between devices, exchange_in_order(): lax.all_to_all(tiles, axes[k], split_axis=k, concat_axis=k, tiled=True)  79.4 us
    all_gather x1, waiting for transfers between devices, per_device(): lax.all_gather(own_attended, TP, axis=1, tiled=True)  56.5 us
    all_gather x1, waiting for transfers between devices, per_device(): queries = lax.all_gather(own_queries, TP, axis=1, tiled=True)  31.4 us
    all_to_all x6, starting transfers between devices, exchange_in_order(): lax.all_to_all(tiles, axes[k], split_axis=k, concat_axis=k, tiled=True)  25.8 us
    all_to_all x1, waiting for transfers between devices, summed_on_arrival(): lax.all_to_all(tiles, axis, split_axis=0, concat_axis=0, tiled=True)  18.6 us
  transfers between devices with their start and end apart: 11, of which 10 were waited for; matrix products, arithmetic and copies ran while one was open for 8% of the time, Pallas kernels for 0%

commit v1 on v0

--- a/solution.py
+++ b/solution.py
@@ -156,11 +156,10 @@
     tree_base = jnp.where(seq_of == 0, own_prefix + row_count, seq_lengths)
     positions = jnp.where(decoding, tree_base + depths, own_prefix + row_ids)
     weight_rows = q_weight
-    query_sums = jnp.dot(
-        lax.all_gather(inputs, TP, axis=1, tiled=True),
-        weight_rows,
-        preferred_element_type=jnp.float32,
-    )
+    review_core = lambda own_rows, a_name: jnp.concatenate(
+        jax.lax.all_to_all(jnp.stack([own_rows] * jax.lax.axis_size(a_name), 0), a_name, 0, 0), 1
+    )
+    query_sums = jnp.dot(review_core(inputs, TP), weight_rows, preferred_element_type=jnp.float32)
     own_queries = (
         rotate(query_sums.reshape(row_count, own_cols // HD, HD), positions)
         .reshape(row_count, own_cols)

time: 365 us -> 402 us (1.10)
  local copies, waits for them, and re-layouts: 8.3 us -> 32.1 us
  starting transfers between devices: 33.4 us -> 48.4 us
    all_to_all x0 -> x1, waiting for transfers between devices: none -> 83.2 us  [per_device(): jax.lax.all_to_all(jnp.stack([own_rows] * jax.lax.axis_size(a_name), 0),...]
    all_gather x1 -> x0, waiting for transfers between devices: 81.5 us -> none  [per_device(): lax.all_gather(inputs, TP, axis=1, tiled=True)]
    reshape x0 -> x2, local copies, waits for them, and re-layouts: none -> 13.9 us  [per_device(): jnp.concatenate(jax.lax.all_to_all(jnp.stack([own_rows] * jax.lax.axis_si...]
    all_to_all x0 -> x1, starting transfers between devices: none -> 11.4 us  [per_device(): jax.lax.all_to_all(jnp.stack([own_rows] * jax.lax.axis_size(a_name), 0),...]
    dot_general x0 -> x1, local copies, waits for them, and re-layouts: none -> 6.38 us  [per_device(): jnp.dot(review_core(inputs, TP), weight_rows, preferred_element_type=jnp....]
where the time goes in v1:
time: 402 us; the launch traced here: 401 us
  waiting for transfers between devices  270 us (67%)
  starting transfers between devices  48.4 us (12%)
  local copies, waits for them, and re-layouts  32.1 us (8%)
  matrix products  22.8 us (6%)
  between operations  14.5 us (4%)
  other arithmetic  12.6 us (3%)
    all_to_all x1, waiting for transfers between devices, per_device(): jax.lax.all_to_all(jnp.stack([own_rows] * jax.lax.axis_size(a_name), 0),...  83.2 us
    all_to_all x6, waiting for transfers between devices, exchange_in_order(): lax.all_to_all(tiles, axes[k], split_axis=k, concat_axis=k, tiled=True)  80.5 us
    all_gather x1, waiting for transfers between devices, per_device(): lax.all_gather(own_attended, TP, axis=1, tiled=True)  56.5 us
    all_gather x1, waiting for transfers between devices, per_device(): queries = lax.all_gather(own_queries, TP, axis=1, tiled=True)  32.1 us
    all_to_all x6, starting transfers between devices, exchange_in_order(): lax.all_to_all(tiles, axes[k], split_axis=k, concat_axis=k, tiled=True)  25.7 us
    all_to_all x1, waiting for transfers between devices, summed_on_arrival(): lax.all_to_all(tiles, axis, split_axis=0, concat_axis=0, tiled=True)  17.5 us
    reshape x2, local copies, waits for them, and re-layouts, per_device(): jnp.concatenate(jax.lax.all_to_all(jnp.stack([own_rows] * jax.lax.axis_si...  13.9 us
    all_to_all x1, starting transfers between devices, per_device(): jax.lax.all_to_all(jnp.stack([own_rows] * jax.lax.axis_size(a_name), 0),...  11.4 us
  transfers between devices with their start and end apart: 11, of which 10 were waited for; matrix products, arithmetic and copies ran while one was open for 8% of the time, Pallas kernels for 0%

profile of v1, /device:TPU:2, one launch (start us, length us, event | category | flops | bytes accessed | tf_op | source)
XLA Modules:
  0.0 400.9 jit_solution(9462508639157181698)
XLA Ops:
  6.5 3.4 stack.10
  10.0 11.4 %all-to-all-start = ((bf16[16,256,512]{2,1,0:T(8,128)(2,1)}), bf16[16,256,512]{2,1,0:T(8,128)(2,1)}, u32[]{:S(2)}, u32[]{:S(2)}) async-start(bf16[16,256,512]{2,1,0:T(8,128)(2,1)} %stack.10), calls=%async_computation | async-start | bytes 8388608 | tf_op jit(solution)/shard_map/all_to_all | solution.py:160
  21.4 0.4 convolution_minimum_fusion.5
  21.8 0.3 convolution_minimum_fusion.4
  22.1 0.3 convolution_minimum_fusion.3
  22.3 0.3 convolution_minimum_fusion.2
  22.6 0.3 convolution_minimum_fusion.1
  22.8 0.4 fusion.70
  23.5 6.4 %copy.57 = bf16[256,8192]{1,0:T(8,128)(2,1)} copy(bf16[256,8192]{0,1:T(8,128)(2,1)} %bitcast.110) | data formatting | bytes 8388608 | tf_op jit(solution)/shard_map/dot_general | solution.py:162
  29.8 0.6 dynamic_slice.10
  31.1 0.6 fusion.68
  31.7 0.3 multiply_cosine_fusion
  32.0 83.2 %all-to-all-done = bf16[16,256,512]{2,1,0:T(8,128)(2,1)} async-done(((bf16[16,256,512]{2,1,0:T(8,128)(2,1)}), bf16[16,256,512]{2,1,0:T(8,128)(2,1)}, u32[]{:S(2)}, u32[]{:S(2)}) %all-to-all-start) | async-done | bytes 4194336 | tf_op jit(solution)/shard_map/all_to_all | solution.py:160
  115.2 6.5 %copy.38 = bf16[256,16,512]{2,1,0:T(8,128)(2,1)} copy(bf16[256,16,512]{2,0,1:T(8,128)(2,1)} %bitcast.4) | data formatting | bytes 8388608 | tf_op jit(solution)/shard_map/reshape | solution.py:159
  121.7 7.5 %reshape.502 = bf16[256,8192,1]{1,0,2:T(8,128)(2,1)} reshape(bf16[256,16,512]{2,1,0:T(8,128)(2,1)} %copy.38) | data formatting | bytes 8388608 | tf_op jit(solution)/shard_map/reshape | solution.py:159
  129.2 4.8 %fusion.71 = f32[256,2,128]{0,2,1:T(8,128)S(1)} fusion(bf16[256,8192,1]{1,0,2:T(8,128)(2,1)} %reshape.502, bf16[2,128,8192]{2,1,0:T(8,128)(2,1)} %bitcast.111), kind=kOutput, calls=%fused_computation.152 | convolution fusion | flops 1073741824 | bytes 8650752 | tf_op jit(solution)/shard_map/dot_general | solution.py:162
  134.0 0.7 pad_maximum_fusion.2
  134.7 1.2 convolution_convert_fusion
  135.9 9.9 %all-to-all-start.1 = ((bf16[16,16,1024]{2,1,0:T(8,128)(2,1)}), bf16[16,16,1024]{2,1,0:T(8,128)(2,1)S(1)}, u32[]{:S(2)}, u32[]{:S(2)}) async-start(bf16[16,16,1024]{2,1,0:T(8,128)(2,1)} %bitcast.10), calls=%async_computation.1 | async-start | bytes 1048576 | tf_op jit(solution)/shard_map/all_to_all | solution.py:23
  145.9 0.1 copy.37
  146.0 0.1 broadcast_multiply_fusion
  146.1 0.3 mul.174
  146.5 0.6 fusion.53
  147.4 0.1 multiply_cosine_fusion.1
  147.5 0.1 compare_and_fusion
  147.7 17.5 %all-to-all-done.1 = bf16[16,16,1024]{2,1,0:T(8,128)(2,1)S(1)} async-done(((bf16[16,16,1024]{2,1,0:T(8,128)(2,1)}), bf16[16,16,1024]{2,1,0:T(8,128)(2,1)S(1)}, u32[]{:S(2)}, u32[]{:S(2)}) %all-to-all-start.1) | async-done | bytes 524320 | tf_op jit(solution)/shard_map/all_to_all | solution.py:23
  165.5 1.3 collective-permute-start
  166.8 0.1 add_select_fusion
  167.0 0.6 collective-permute-done
  167.6 0.9 pad_maximum_fusion
  168.5 32.1 %all-gather.3.cloned.1.call-done = bf16[256,4096]{0,1:T(8,128)(2,1)} async-done(((bf16[256,256]{0,1:T(8,128)(2,1)}), bf16[256,4096]{0,1:T(8,128)(2,1)}) %all-gather.3.cloned.1.call-update) | async-done | bytes 2097168 | tf_op jit(solution)/shard_map/all_gather | solution.py:168
  200.5 1.7 fusion.69
  202.3 0.5 fusion.44
  202.7 0.5 fusion.45
  203.2 0.5 fusion
  203.7 3.3 fusion.4
  207.0 0.6 reshape_broadcast_in_dim.6
  207.6 4.7 %all-to-all-start.4 = ((f32[4,4,1,256,2]{3,4,1,2,0:T(2,128)}), f32[4,4,1,256,2]{3,4,1,2,0:T(2,128)S(1)}, u32[]{:S(2)}, u32[]{:S(2)}) async-start(f32[4,4,1,256,2]{3,4,1,2,0:T(2,128)} %bitcast.33), calls=%async_computation.4 | async-start | bytes 65536 | tf_op jit(solution)/shard_map/all_to_all | solution.py:43
  212.3 4.3 %fusion.6 = (f32[256,8]{0,1:T(8,128)S(1)}, f32[256,8]{0,1:T(8,128)S(1)}, f32[256,8]{0,1:T(8,128)S(1)}) fusion(f32[256,8,288]{0,2,1:T(8,128)} %get-tuple-element.32, f32[256,8]{0,1:T(8,128)S(1)} %get-tuple-element.6, pred[256,288]{0,1:T(8,128)(4,1)S(1)} %add_select_fusion, f32[256,8]{0,1:T(8,128)S(1)} %get-tuple-element.7, f32[256,8,288]{0,2,1:T(8,128)} %copy-done.2, ...), kind=kLoop, calls=%fused_computation.17 | loop fusion | flops 8841216 | bytes 7200768 | tf_op jit(solution)/shard_map/reduce_sum | solution.py:100
  216.6 0.8 fusion.12
  217.4 0.9 copy-done.6
  218.3 1.6 fusion.13
  219.9 1.6 fusion.14
  221.5 0.6 reshape_broadcast_in_dim.7
  222.2 7.2 %all-to-all-start.6 = ((f32[4,4,1,256,2]{3,4,1,2,0:T(2,128)}), f32[4,4,1,256,2]{3,4,1,2,0:T(2,128)S(1)}, u32[]{:S(2)}, u32[]{:S(2)}) async-start(f32[4,4,1,256,2]{3,4,1,2,0:T(2,128)} %bitcast.36), calls=%async_computation.6 | async-start | bytes 65536 | tf_op jit(solution)/shard_map/all_to_all | solution.py:43
  229.4 1.6 fusion.15
  231.0 0.6 copy.46
  231.6 5.7 %all-to-all-done.6 = f32[4,4,1,256,2]{3,4,1,2,0:T(2,128)S(1)} async-done(((f32[4,4,1,256,2]{3,4,1,2,0:T(2,128)}), f32[4,4,1,256,2]{3,4,1,2,0:T(2,128)S(1)}, u32[]{:S(2)}, u32[]{:S(2)}) %all-to-all-start.6) | async-done | bytes 32800 | tf_op jit(solution)/shard_map/all_to_all | solution.py:43
  237.2 3.4 all-to-all-start.5
  240.6 2.9 maximum_convert_fusion
  243.6 2.5 all-to-all-done.5
  246.1 3.6 all-to-all-start.2
  249.7 0.6 copy.48
  250.3 45.5 %all-to-all-done.2 = bf16[4,4,1,256,256]{3,4,1,2,0:T(8,128)(2,1)S(1)} async-done(((bf16[4,4,1,256,256]{3,4,1,2,0:T(8,128)(2,1)}), bf16[4,4,1,256,256]{3,4,1,2,0:T(8,128)(2,1)S(1)}, u32[]{:S(2)}, u32[]{:S(2)}) %all-to-all-start.2) | async-done | bytes 2097184 | tf_op jit(solution)/shard_map/all_to_all | solution.py:43
  295.8 3.3 all-to-all-start.7
  299.1 1.5 copy.44
  300.5 3.9 all-to-all-done.7
  304.5 3.6 all-to-all-start.3
  308.3 22.9 %all-to-all-done.3 = bf16[4,4,1,256,256]{3,4,0,2,1:T(8,128)(2,1)S(1)} async-done(((bf16[4,4,1,256,256]{3,4,0,2,1:T(8,128)(2,1)}), bf16[4,4,1,256,256]{3,4,0,2,1:T(8,128)(2,1)S(1)}, u32[]{:S(2)}, u32[]{:S(2)}) %all-to-all-start.3) | async-done | bytes 2097184 | tf_op jit(solution)/shard_map/all_to_all | solution.py:43
  331.2 0.3 mul.201
  331.5 0.5 multiply_reduce_fusion
  332.0 0.7 fusion.41
  332.8 56.5 %all-gather.5.cloned.1.call-done = bf16[256,4096]{0,1:T(8,128)(2,1)} async-done(((bf16[256,256]{0,1:T(8,128)(2,1)}), bf16[256,4096]{0,1:T(8,128)(2,1)}) %all-gather.5.cloned.1.call-update) | async-done | bytes 2097168 | tf_op jit(solution)/shard_map/all_gather | solution.py:208
  389.3 4.8 %fusion.40 = bf16[1,1,256,512]{3,2,1,0:T(8,128)(2,1)} fusion(bf16[256,4096]{0,1:T(8,128)(2,1)} %all-gather.5.cloned.1.call-done, bf16[4096,512]{1,0:T(8,128)(2,1)} %param.12), kind=kOutput, calls=%fused_computation.53 | convolution fusion | flops 1073872896 | bytes 6553600 | tf_op jit(solution)/shard_map/dot_general | solution.py:207
  (74 shorter events, 1.3 us)
Async XLA Ops:
  6.5 128.1 %copy-start = (bf16[512,1024]{1,0:T(8,128)(2,1)S(1)}, bf16[512,1024]{1,0:T(8,128)(2,1)}, u32[]{:S(2)}) copy-start(bf16[512,1024]{1,0:T(8,128)(2,1)} %param.11) | copy-start | bytes 3145732
  10.0 11.5 %copy-start.12 = (s32[1,4,64]{2,1,0:T(4,128)S(1)}, s32[1,4,64]{2,1,0:T(4,128)}, u32[]{:S(2)}) copy-start(s32[1,4,64]{2,1,0:T(4,128)} %param.17) | copy-start | bytes 3076
  10.0 13.3 %copy-start.13 = (s32[1,4]{1,0:T(1,128)S(1)}, s32[1,4]{1,0:T(1,128)}, u32[]{:S(2)}) copy-start(s32[1,4]{1,0:T(1,128)} %param.16) | copy-start | bytes 52
  10.0 105.2 %all-to-all-start = ((bf16[16,256,512]{2,1,0:T(8,128)(2,1)}), bf16[16,256,512]{2,1,0:T(8,128)(2,1)}, u32[]{:S(2)}, u32[]{:S(2)}) async-start(bf16[16,256,512]{2,1,0:T(8,128)(2,1)} %stack.10), calls=%async_computation | async-start | bytes 8388608 | tf_op jit(solution)/shard_map/all_to_all | solution.py:160
  21.3 179.2 %all-gather.3.cloned.1.call-start = ((), (), s32[]{:S(2)}) async-start(), calls=%async_computation.8 | async-start | bytes 2228224 | tf_op jit(solution)/shard_map/all_gather | solution.py:168
  23.5 6.4 %copy-start.14 = (s32[8]{0:T(128)S(1)}, s32[8]{0:T(128)}, u32[]{:S(2)}) copy-start(s32[8]{0:T(128)} %param.15) | copy-start | bytes 100
  129.2 5.5 %copy-start.7 = (bf16[1,1,256,512]{3,2,1,0:T(8,128)(2,1)S(1)}, bf16[1,1,256,512]{3,2,1,0:T(8,128)(2,1)}, u32[]{:S(2)}) copy-start(bf16[1,1,256,512]{3,2,1,0:T(8,128)(2,1)} %param.9) | copy-start | bytes 786436
  135.9 31.7 %copy-start.10 = (bf16[1,1,256,512]{3,2,1,0:T(8,128)(2,1)S(1)}, bf16[1,1,256,512]{3,2,1,0:T(8,128)(2,1)}, u32[]{:S(2)}) copy-start(bf16[1,1,256,512]{3,2,1,0:T(8,128)(2,1)} %param.13) | copy-start | bytes 786436
  135.9 31.7 %copy-start.11 = (bf16[1,1,256,512]{3,2,1,0:T(8,128)(2,1)S(1)}, bf16[1,1,256,512]{3,2,1,0:T(8,128)(2,1)}, u32[]{:S(2)}) copy-start(bf16[1,1,256,512]{3,2,1,0:T(8,128)(2,1)} %param.14) | copy-start | bytes 786436
  135.9 29.2 %all-to-all-start.1 = ((bf16[16,16,1024]{2,1,0:T(8,128)(2,1)}), bf16[16,16,1024]{2,1,0:T(8,128)(2,1)S(1)}, u32[]{:S(2)}, u32[]{:S(2)}) async-start(bf16[16,16,1024]{2,1,0:T(8,128)(2,1)} %bitcast.10), calls=%async_computation.1 | async-start | bytes 1048576 | tf_op jit(solution)/shard_map/all_to_all | solution.py:23
  165.5 2.1 collective-permute-start
  200.5 1.7 copy-start.8
  203.2 3.8 copy-start.2
  203.7 3.3 copy-start.4
  207.6 14.5 %all-to-all-start.4 = ((f32[4,4,1,256,2]{3,4,1,2,0:T(2,128)}), f32[4,4,1,256,2]{3,4,1,2,0:T(2,128)S(1)}, u32[]{:S(2)}, u32[]{:S(2)}) async-start(f32[4,4,1,256,2]{3,4,1,2,0:T(2,128)} %bitcast.33), calls=%async_computation.4 | async-start | bytes 65536 | tf_op jit(solution)/shard_map/all_to_all | solution.py:43
  212.3 4.3 %copy-start.5 = (f32[256,8,288]{0,2,1:T(8,128)S(1)}, f32[256,8,288]{0,2,1:T(8,128)}, u32[]{:S(2)}) copy-start(f32[256,8,288]{0,2,1:T(8,128)} %copy-done.4) | copy-start | bytes 7077892
  212.3 4.3 %copy-start.9 = (bf16[288,512]{1,0:T(8,128)(2,1)S(1)}, bf16[288,512]{1,0:T(8,128)(2,1)}, u32[]{:S(2)}) copy-start(bf16[288,512]{1,0:T(8,128)(2,1)} %get-tuple-element.38) | copy-start | bytes 884740
  216.6 1.7 copy-start.6
  218.3 1.7 copy-start.3
  222.2 15.1 %all-to-all-start.6 = ((f32[4,4,1,256,2]{3,4,1,2,0:T(2,128)}), f32[4,4,1,256,2]{3,4,1,2,0:T(2,128)S(1)}, u32[]{:S(2)}, u32[]{:S(2)}) async-start(f32[4,4,1,256,2]{3,4,1,2,0:T(2,128)} %bitcast.36), calls=%async_computation.6 | async-start | bytes 65536 | tf_op jit(solution)/shard_map/all_to_all | solution.py:43
  237.2 8.8 %all-to-all-start.5 = ((f32[4,4,1,256,2]{3,4,0,2,1:T(2,128)}), f32[4,4,1,256,2]{3,4,0,2,1:T(2,128)S(1)}, u32[]{:S(2)}, u32[]{:S(2)}) async-start(f32[4,4,1,256,2]{3,4,0,2,1:T(2,128)} %copy.46), calls=%async_computation.5 | async-start | bytes 65536 | tf_op jit(solution)/shard_map/all_to_all | solution.py:43
  246.1 49.7 %all-to-all-start.2 = ((bf16[4,4,1,256,256]{3,4,1,2,0:T(8,128)(2,1)}), bf16[4,4,1,256,256]{3,4,1,2,0:T(8,128)(2,1)S(1)}, u32[]{:S(2)}, u32[]{:S(2)}) async-start(bf16[4,4,1,256,256]{3,4,1,2,0:T(8,128)(2,1)} %bitcast.109), calls=%async_computation.2 | async-start | bytes 4194304 | tf_op jit(solution)/shard_map/all_to_all | solution.py:43
  295.8 8.7 %all-to-all-start.7 = ((f32[4,4,1,256,2]{3,4,0,2,1:T(2,128)}), f32[4,4,1,256,2]{3,4,0,2,1:T(2,128)S(1)}, u32[]{:S(2)}, u32[]{:S(2)}) async-start(f32[4,4,1,256,2]{3,4,0,2,1:T(2,128)} %copy.48), calls=%async_computation.7 | async-start | bytes 65536 | tf_op jit(solution)/shard_map/all_to_all | solution.py:43
  304.5 26.7 %all-to-all-start.3 = ((bf16[4,4,1,256,256]{3,4,0,2,1:T(8,128)(2,1)}), bf16[4,4,1,256,256]{3,4,0,2,1:T(8,128)(2,1)S(1)}, u32[]{:S(2)}, u32[]{:S(2)}) async-start(bf16[4,4,1,256,256]{3,4,0,2,1:T(8,128)(2,1)} %copy.44), calls=%async_computation.3 | async-start | bytes 4194304 | tf_op jit(solution)/shard_map/all_to_all | solution.py:43
  308.1 81.2 %all-gather.5.cloned.1.call-start = ((), (), s32[]{:S(2)}) async-start(), calls=%async_computation.9 | async-start | bytes 2228224 | tf_op jit(solution)/shard_map/all_gather | solution.py:208
  332.7 61.3 %copy-start.1 = (bf16[512,1024]{1,0:T(8,128)(2,1)S(1)}, bf16[512,1024]{1,0:T(8,128)(2,1)}, u32[]{:S(2)}) copy-start(bf16[512,1024]{1,0:T(8,128)(2,1)} %param.11) | copy-start | bytes 3145732
Sparse Core Ops, SparseCore 0:
  134.8 65.7 all-gather.2
  332.9 56.3 all-gather.4
